TPU v7x, 32 devices: a whole 2x2x4 slice. The times are simulated.
32 devices in a mesh: batch: 8 (over y, x, core), chan: 4 (over z).
Axes of the slice: x: 2, y: 2, z: 4, core: 2. Of those that a mesh axis runs over, the one named last changes fastest.
Arguments:
- images: bfloat16 [64, 14, 14, 4096], P('batch', None, None, 'chan'), may hold values from -12 to 12, as said below
- reduce_weight: bfloat16 [4096, 1024], P(None, 'chan'), may hold values from -0.09375 to 0.09375
- reduce_gain: float32 [1024], P('chan'), may hold values from 0.25 to 1.75
- reduce_bias: float32 [1024], P('chan'), may hold values from -0.5 to 0.5
- spatial_weight: bfloat16 [3, 3, 1024, 1024], P(None, None, None, 'chan'), may hold values from -0.0625 to 0.0625
- spatial_gain: float32 [1024], P('chan'), may hold values from 0.25 to 1.75
- spatial_bias: float32 [1024], P('chan'), may hold values from -0.5 to 0.5
- expand_weight: bfloat16 [1024, 4096], P(None, 'chan'), may hold values from -0.1875 to 0.1875
- expand_gain: float32 [4096], P('chan'), may hold values from 0.25 to 1.75
- expand_bias: float32 [4096], P('chan'), may hold values from -0.5 to 0.5
Outputs:
- block_out: bfloat16 [64, 14, 14, 4096], P('batch', None, None, 'chan')
Inputs may be any that keep to these rules, and one draw needn't show every extreme that they name: In the images, the per-channel mean and scale differ from one block of 8 images to the next.
All inputs are finite; a program needn't handle non-finite values.
Results may differ from a plain program's by a relative error of at most 0.0047.
Values may be sent and summed in bfloat16 or wider, within the bound.
No kernel may reach another device: no remote copies, remote signals or barrier semaphores. Data moves between devices by JAX's collectives and lax.ppermute only.
A program may use at most 128 MiB of HBM per device.

v0:
```python
import jax
import jax.numpy as jnp
from jax import lax
from jax.sharding import PartitionSpec as P

eps = 0.001


def totals(parts):
    return lax.psum((parts[0],), "batch")


def batch_norm(values, gain, bias, count):
    (total,) = totals((jnp.sum(values, axis=0),))
    mean = total / count
    centred = values - mean
    (spread,) = totals((jnp.sum(centred * centred, axis=0),))
    var = spread / count
    return centred * (gain / jnp.sqrt(var + eps)) + bias


def body(
    images,
    reduce_weight,
    reduce_gain,
    reduce_bias,
    spatial_weight,
    spatial_gain,
    spatial_bias,
    expand_weight,
    expand_gain,
    expand_bias,
):
    imgs, side = (images.shape[0], images.shape[1])
    rows = imgs * side * side
    count = rows * lax.axis_size("batch")
    mid_local = reduce_weight.shape[1]
    out_local = expand_weight.shape[1]
    own_rows = lax.all_to_all(reduce_weight, "chan", split_axis=0, concat_axis=1, tiled=True)
    partial_first = jnp.dot(
        images.reshape(rows, out_local), own_rows, preferred_element_type=jnp.float32
    )
    first = lax.psum_scatter(partial_first, "chan", scatter_dimension=1, tiled=True)
    act_one = jnp.maximum(batch_norm(first, reduce_gain, reduce_bias, count), 0.0).astype(
        jnp.bfloat16
    )
    act_one = act_one.reshape(imgs, side, side, mid_local)
    total = jnp.zeros((rows, mid_local), jnp.float32)
    piece = lax.all_gather(act_one, "chan", axis=3, tiled=True)
    width = piece.shape[-1]
    padded = jnp.pad(piece, ((0, 0), (1, 1), (1, 1), (0, 0)))
    for row_tap in range(3):
        for col_tap in range(3):
            window = padded[:, row_tap : row_tap + side, col_tap : col_tap + side, :].reshape(
                rows, width
            )
            block = spatial_weight[row_tap, col_tap]
            total = total + jnp.dot(window, block, preferred_element_type=jnp.float32)
    act_two = jnp.maximum(batch_norm(total, spatial_gain, spatial_bias, count), 0.0).astype(
        jnp.bfloat16
    )
    block = expand_weight
    third = jnp.dot(
        lax.all_gather(act_two, "chan", axis=1, tiled=True),
        block,
        preferred_element_type=jnp.float32,
    )
    normed = batch_norm(third, expand_gain, expand_bias, count)
    summed = normed + images.reshape(rows, out_local).astype(jnp.float32)
    return jnp.maximum(summed, 0.0).astype(jnp.bfloat16).reshape(imgs, side, side, out_local)


def solution(mesh):
    in_specs = (
        P("batch", None, None, "chan"),
        P(None, "chan"),
        P("chan"),
        P("chan"),
        P(None, None, None, "chan"),
        P("chan"),
        P("chan"),
        P(None, "chan"),
        P("chan"),
        P("chan"),
    )
    out_specs = P("batch", None, None, "chan")
    return jax.shard_map(body, mesh=mesh, in_specs=in_specs, out_specs=out_specs, check_vma=False)
```

profile of v0, /device:TPU:0, one launch (start us, length us, event | category | flops | bytes accessed | tf_op | source)
XLA Modules:
  0.0 540.0 jit_solution(18199424458085482704)
XLA Ops:
  6.5 6.5 %all-to-all-start = ((bf16[4,1024,256]{2,1,0:T(8,128)(2,1)}), bf16[4,1024,256]{2,1,0:T(8,128)(2,1)}, u32[]{:S(2)}, u32[]{:S(2)}) async-start(bf16[4,1024,256]{2,1,0:T(8,128)(2,1)} %bitcast.45), calls=%async_computation | async-start | bytes 4194304 | tf_op jit(solution)/shard_map/all_to_all | solution.py:39
  13.0 5.5 %copy.15 = bf16[8,14,14,1024]{3,2,1,0:T(8,128)(2,1)} copy(bf16[8,14,14,1024]{3,0,2,1:T(8,128)(2,1)} %param.10) | data formatting | bytes 6422528 | tf_op args[0]
  18.5 5.6 %reshape.49 = bf16[1568,1024]{1,0:T(8,128)(2,1)} reshape(bf16[8,14,14,1024]{3,2,1,0:T(8,128)(2,1)} %copy.15) | data formatting | bytes 6422528 | tf_op jit(solution)/shard_map/reshape | solution.py:41
  24.1 37.2 %all-to-all-done = bf16[4,1024,256]{2,1,0:T(8,128)(2,1)} async-done(((bf16[4,1024,256]{2,1,0:T(8,128)(2,1)}), bf16[4,1024,256]{2,1,0:T(8,128)(2,1)}, u32[]{:S(2)}, u32[]{:S(2)}) %all-to-all-start) | async-done | bytes 2097184 | tf_op jit(solution)/shard_map/all_to_all | solution.py:39
  61.3 4.0 copy.16
  65.3 8.8 %fusion.21 = f32[1568,1024]{1,0:T(8,128)} fusion(bf16[1568,1024]{1,0:T(8,128)(2,1)} %reshape.49, bf16[1024,1024]{0,1:T(8,128)(2,1)} %bitcast.46), kind=kOutput, calls=%fused_computation.49 | convolution fusion | flops 3288334336 | bytes 11730944 | tf_op jit(solution)/shard_map/dot_general | solution.py:40
  74.2 112.1 %reduce-scatter.2.cloned.1.call-done = f32[1568,256]{1,0:T(8,128)} async-done(((f32[1568,1024]{1,0:T(8,128)}), f32[1568,256]{1,0:T(8,128)}) %reduce-scatter.2.cloned.1.call-update) | async-done | bytes 1605648 | tf_op jit(solution)/shard_map/reduce_scatter | solution.py:43
  187.9 13.5 %psum.42 = f32[256]{0:T(256)S(1)} all-reduce(f32[256]{0:T(256)S(1)} %reduce_sum.54), channel_id=1, replica_groups=mesh['batch'=8,'chan'=4] {'batch'}, use_global_device_ids=true, to_apply=%region_2.0 | all-reduce | flops 256 | bytes 2048 | tf_op jit(solution)/shard_map/psum | solution.py:10
  203.1 11.8 %psum.43 = f32[256]{0:T(256)S(1)} all-reduce(f32[256]{0:T(256)S(1)} %multiply_reduce_fusion.2), channel_id=1, replica_groups=mesh['batch'=8,'chan'=4] {'batch'}, use_global_device_ids=true, to_apply=%region_4.0 | all-reduce | flops 256 | bytes 2048 | tf_op jit(solution)/shard_map/psum | solution.py:10
  218.0 70.6 %all-gather.3.cloned.1.call-done = bf16[8,14,14,1024]{3,2,1,0:T(8,128)(2,1)} async-done(((bf16[8,14,14,256]{3,2,1,0:T(8,128)(2,1)}), bf16[8,14,14,1024]{3,2,1,0:T(8,128)(2,1)}) %all-gather.3.cloned.1.call-update) | async-done | bytes 3211280 | tf_op jit(solution)/shard_map/all_gather | solution.py:49
  288.6 23.7 %pad_slice_fusion = (bf16[8,14,14,1024]{3,2,1,0:T(8,128)(2,1)}, bf16[8,14,14,1024]{3,2,1,0:T(8,128)(2,1)}, bf16[8,14,14,1024]{3,2,1,0:T(8,128)(2,1)}, bf16[8,14,...) fusion(bf16[8,14,14,1024]{3,2,1,0:T(8,128)(2,1)} %all-gather.3., ...), kind=kLoop, calls=%fused_computation.10 | loop fusion | bytes 28901376 | tf_op jit(solution)/shard_map/slice | solution.py:54
  312.3 5.7 %reshape.59 = bf16[1568,1024]{1,0:T(8,128)(2,1)} reshape(bf16[8,14,14,1024]{3,2,1,0:T(8,128)(2,1)} %get-tuple-element.5) | data formatting | bytes 6422528 | tf_op jit(solution)/shard_map/reshape | solution.py:54
  318.1 5.7 %reshape.52 = bf16[1568,1024]{1,0:T(8,128)(2,1)} reshape(bf16[8,14,14,1024]{3,2,1,0:T(8,128)(2,1)} %get-tuple-element.6) | data formatting | bytes 6422528 | tf_op jit(solution)/shard_map/reshape | solution.py:54
  323.7 5.6 %reshape.53 = bf16[1568,1024]{1,0:T(8,128)(2,1)} reshape(bf16[8,14,14,1024]{3,2,1,0:T(8,128)(2,1)} %get-tuple-element.7) | data formatting | bytes 6422528 | tf_op jit(solution)/shard_map/reshape | solution.py:54
  329.4 5.7 %reshape.54 = bf16[1568,1024]{1,0:T(8,128)(2,1)} reshape(bf16[8,14,14,1024]{3,2,1,0:T(8,128)(2,1)} %get-tuple-element.8) | data formatting | bytes 6422528 | tf_op jit(solution)/shard_map/reshape | solution.py:54
  335.0 5.7 %reshape.56 = bf16[1568,1024]{1,0:T(8,128)(2,1)} reshape(bf16[8,14,14,1024]{3,2,1,0:T(8,128)(2,1)} %get-tuple-element.9) | data formatting | bytes 6422528 | tf_op jit(solution)/shard_map/reshape | solution.py:54
  340.7 5.6 %reshape.57 = bf16[1568,1024]{1,0:T(8,128)(2,1)} reshape(bf16[8,14,14,1024]{3,2,1,0:T(8,128)(2,1)} %get-tuple-element.10) | data formatting | bytes 6422528 | tf_op jit(solution)/shard_map/reshape | solution.py:54
  346.3 5.6 %reshape.58 = bf16[1568,1024]{1,0:T(8,128)(2,1)} reshape(bf16[8,14,14,1024]{3,2,1,0:T(8,128)(2,1)} %get-tuple-element.11) | data formatting | bytes 6422528 | tf_op jit(solution)/shard_map/reshape | solution.py:54
  352.0 5.7 %reshape.51 = bf16[1568,1024]{1,0:T(8,128)(2,1)} reshape(bf16[8,14,14,1024]{3,2,1,0:T(8,128)(2,1)} %get-tuple-element.12) | data formatting | bytes 6422528 | tf_op jit(solution)/shard_map/reshape | solution.py:54
  368.5 5.6 %reshape.55 = bf16[1568,1024]{1,0:T(8,128)(2,1)} reshape(bf16[8,14,14,1024]{3,2,1,0:T(8,128)(2,1)} %all-gather.3.cloned.1.call-done) | data formatting | bytes 6422528 | tf_op jit(solution)/shard_map/reshape | solution.py:54
  374.2 3.7 convolution_add_fusion.4
  384.6 3.3 fusion.19
  387.8 13.6 %psum.44 = f32[256]{0:T(256)S(1)} all-reduce(f32[256]{0:T(256)S(1)} %get-tuple-element.13), channel_id=1, replica_groups=mesh['batch'=8,'chan'=4] {'batch'}, use_global_device_ids=true, to_apply=%region_6.7 | all-reduce | flops 256 | bytes 2048 | tf_op jit(solution)/shard_map/psum | solution.py:10
  403.1 11.8 %psum.45 = f32[256]{0:T(256)S(1)} all-reduce(f32[256]{0:T(256)S(1)} %multiply_reduce_fusion.1), channel_id=1, replica_groups=mesh['batch'=8,'chan'=4] {'batch'}, use_global_device_ids=true, to_apply=%region_8.9 | all-reduce | flops 256 | bytes 2048 | tf_op jit(solution)/shard_map/psum | solution.py:10
  417.5 61.0 %all-gather.5.cloned.1.call-done = bf16[1568,1024]{1,0:T(8,128)(2,1)} async-done(((bf16[1568,256]{1,0:T(8,128)(2,1)}), bf16[1568,1024]{1,0:T(8,128)(2,1)}) %all-gather.5.cloned.1.call-update) | async-done | bytes 3211280 | tf_op jit(solution)/shard_map/all_gather | solution.py:64
  478.5 7.4 %fusion.20 = (f32[1024]{0:T(1024)S(1)}, f32[1568,1024]{1,0:T(8,128)}) fusion(bf16[1568,1024]{1,0:T(8,128)(2,1)} %all-gather.5.cloned.1.call-done, bf16[1024,1024]{1,0:T(8,128)(2,1)S(1)} %copy-done), kind=kOutput, calls=%fused_computation.48 | convolution fusion | flops 3289938944 | bytes 11735040 | tf_op jit(solution)/shard_map/dot_general | solution.py:63
  485.9 13.6 %psum.46 = f32[1024]{0:T(1024)S(1)} all-reduce(f32[1024]{0:T(1024)S(1)} %get-tuple-element.15), channel_id=1, replica_groups=mesh['batch'=8,'chan'=4] {'batch'}, use_global_device_ids=true, to_apply=%region_10.11 | all-reduce | flops 1024 | bytes 8192 | tf_op jit(solution)/shard_map/psum | solution.py:10
  499.5 3.5 multiply_reduce_fusion
  503.1 11.8 %psum.47 = f32[1024]{0:T(1024)S(1)} all-reduce(f32[1024]{0:T(1024)S(1)} %multiply_reduce_fusion), channel_id=1, replica_groups=mesh['batch'=8,'chan'=4] {'batch'}, use_global_device_ids=true, to_apply=%region_12.13 | all-reduce | flops 1024 | bytes 8192 | tf_op jit(solution)/shard_map/psum | solution.py:10
  514.9 7.0 %maximum_convert_fusion = bf16[1568,1024]{1,0:T(8,128)(2,1)} fusion(bf16[1568,1024]{1,0:T(8,128)(2,1)} %reshape.49, f32[1568,1024]{1,0:T(8,128)} %get-tuple-element.16, f32[1024]{0:T(1024)S(1)} %copy-done.8, f32[1024]{0:T(1024)S(1)} %rsqrt_multiply_fusion, f32[1024]{0:T(1024)S(1)} %broadcast_multiply_fusion), kind=kLoop, calls=%fused_computation | loop fusion | flops 11239424 | bytes 12857344 | tf_op jit(solution)/shard_map/convert_element_type | solution.py:70
  521.8 5.6 %reshape.60 = bf16[8,14,14,1024]{3,2,1,0:T(8,128)(2,1)} reshape(bf16[1568,1024]{1,0:T(8,128)(2,1)} %maximum_convert_fusion) | data formatting | bytes 6422528 | tf_op jit(solution)/shard_map/reshape | solution.py:70
  527.5 6.0 %copy.17 = bf16[8,14,14,1024]{3,0,2,1:T(8,128)(2,1)} copy(bf16[8,14,14,1024]{3,2,1,0:T(8,128)(2,1)} %reshape.60) | data formatting | bytes 6422528 | tf_op jit(solution)/shard_map/reshape | solution.py:70
  (53 shorter events, 28.2 us)
Async XLA Ops:
  6.5 471.9 %copy-start = (bf16[1024,1024]{1,0:T(8,128)(2,1)S(1)}, bf16[1024,1024]{1,0:T(8,128)(2,1)}, u32[]{:S(2)}) copy-start(bf16[1024,1024]{1,0:T(8,128)(2,1)} %param.17) | copy-start | bytes 6291460
  6.5 54.8 %all-to-all-start = ((bf16[4,1024,256]{2,1,0:T(8,128)(2,1)}), bf16[4,1024,256]{2,1,0:T(8,128)(2,1)}, u32[]{:S(2)}, u32[]{:S(2)}) async-start(bf16[4,1024,256]{2,1,0:T(8,128)(2,1)} %bitcast.45), calls=%async_computation | async-start | bytes 4194304 | tf_op jit(solution)/shard_map/all_to_all | solution.py:39
  13.0 173.3 %reduce-scatter.2.cloned.1.call-start = ((), (), s32[]{:S(2)}) async-start(), calls=%async_computation.2 | async-start | bytes 8028160 | tf_op jit(solution)/shard_map/reduce_scatter | solution.py:43
  74.1 140.8 %copy-start.12 = (f32[256]{0:T(256)S(1)}, f32[256]{0:T(256)}, u32[]{:S(2)}) copy-start(f32[256]{0:T(256)} %param.12) | copy-start | bytes 3076
  74.1 140.8 %copy-start.10 = (f32[256]{0:T(256)S(1)}, f32[256]{0:T(256)}, u32[]{:S(2)}) copy-start(f32[256]{0:T(256)} %param.13) | copy-start | bytes 3076
  74.2 214.5 %all-gather.3.cloned.1.call-start = ((), (), s32[]{:S(2)}) async-start(), calls=%async_computation.3 | async-start | bytes 4587520 | tf_op jit(solution)/shard_map/all_gather | solution.py:49
  217.8 260.7 %all-gather.5.cloned.1.call-start = ((), (), s32[]{:S(2)}) async-start(), calls=%async_computation.4 | async-start | bytes 4014080 | tf_op jit(solution)/shard_map/all_gather | solution.py:64
  357.6 3.2 copy-start.7
  360.8 2.2 copy-start.6
  363.0 2.2 copy-start.5
  374.2 3.7 copy-start.4
  377.9 2.2 copy-start.3
  380.1 2.2 copy-start.2
  382.3 2.2 copy-start.1
  384.5 30.4 %copy-start.13 = (f32[256]{0:T(256)S(1)}, f32[256]{0:T(256)}, u32[]{:S(2)}) copy-start(f32[256]{0:T(256)} %param.15) | copy-start | bytes 3076
  384.6 30.4 %copy-start.11 = (f32[256]{0:T(256)S(1)}, f32[256]{0:T(256)}, u32[]{:S(2)}) copy-start(f32[256]{0:T(256)} %param.16) | copy-start | bytes 3076
  499.5 15.4 %copy-start.9 = (f32[1024]{0:T(1024)S(1)}, f32[1024]{0:T(1024)}, u32[]{:S(2)}) copy-start(f32[1024]{0:T(1024)} %param.18) | copy-start | bytes 12292
  499.5 15.4 %copy-start.8 = (f32[1024]{0:T(1024)S(1)}, f32[1024]{0:T(1024)}, u32[]{:S(2)}) copy-start(f32[1024]{0:T(1024)} %param.19) | copy-start | bytes 12292
Sparse Core Ops, SparseCore 0:
  74.3 111.9 reduce-scatter.1
  217.9 70.6 all-gather.2
  417.6 60.7 all-gather.4
where the time goes:
time: 542 us; the launch traced here: 540 us
  waiting for transfers between devices  281 us (52%)
  local copies, waits for them, and re-layouts  103 us (19%)
  blocking collectives  76.2 us (14%)
  matrix products  40.5 us (7%)
  other arithmetic  19.7 us (4%)
  between operations  13.3 us (2%)
  starting transfers between devices  6.74 us (1%)
    reduce_scatter x1, waiting for transfers between devices, body(): lax.psum_scatter(partial_first, 'chan', scatter_dimension=1, tiled=True)  112 us
    psum x6, blocking collectives, totals(): return lax.psum((parts[0],), 'batch')  76.2 us
    all_gather x1, waiting for transfers between devices, body(): piece = lax.all_gather(act_one, 'chan', axis=3, tiled=True)  70.6 us
    all_gather x1, waiting for transfers between devices, body(): lax.all_gather(act_two, 'chan', axis=1, tiled=True)  61 us
    reshape x9, local copies, waits for them, and re-layouts, body(): padded[:, row_tap:row_tap + side, col_tap:col_tap + side, :]  50.9 us
    all_to_all x1, waiting for transfers between devices, body(): lax.all_to_all(reduce_weight, 'chan', split_axis=0, concat_axis=1, tiled=...  37.2 us
    dot_general x9, matrix products, body(): total = total + jnp.dot(window, block, preferred_element_type=jnp.float32)  24.4 us
    slice x1, local copies, waits for them, and re-layouts, body(): padded[:, row_tap:row_tap + side, col_tap:col_tap + side, :]  23.7 us
  transfers between devices with their start and end apart: 4, of which 4 were waited for; matrix products, arithmetic and copies ran while one was open for 2% of the time, Pallas kernels for 0%

commit v1 on v0

--- a/solution.py
+++ b/solution.py
@@ -36,7 +36,12 @@
     count = rows * lax.axis_size("batch")
     mid_local = reduce_weight.shape[1]
     out_local = expand_weight.shape[1]
-    own_rows = lax.all_to_all(reduce_weight, "chan", split_axis=0, concat_axis=1, tiled=True)
+    own_rows = jnp.concatenate(
+        lax.all_to_all(
+            jnp.stack(jnp.split(reduce_weight, lax.axis_size("chan"), axis=0)), "chan", 0, 0
+        ),
+        axis=1,
+    )
     partial_first = jnp.dot(
         images.reshape(rows, out_local), own_rows, preferred_element_type=jnp.float32
     )

time: 542 us -> 550 us (1.015)
    unnamed x29 -> x33, local copies, waits for them, and re-layouts: 5.56 us -> 11.9 us
where the time goes in v1:
time: 550 us; the launch traced here: 548 us
  waiting for transfers between devices  281 us (51%)
  local copies, waits for them, and re-layouts  108 us (20%)
  blocking collectives  76.2 us (14%)
  matrix products  40.5 us (7%)
  other arithmetic  22.7 us (4%)
  between operations  13.4 us (2%)
  starting transfers between devices  6.61 us (1%)
    reduce_scatter x1, waiting for transfers between devices, body(): lax.psum_scatter(partial_first, 'chan', scatter_dimension=1, tiled=True)  112 us
    psum x6, blocking collectives, totals(): return lax.psum((parts[0],), 'batch')  76.2 us
    all_gather x1, waiting for transfers between devices, body(): piece = lax.all_gather(act_one, 'chan', axis=3, tiled=True)  70.5 us
    all_gather x1, waiting for transfers between devices, body(): lax.all_gather(act_two, 'chan', axis=1, tiled=True)  60.9 us
    reshape x9, local copies, waits for them, and re-layouts, body(): padded[:, row_tap:row_tap + side, col_tap:col_tap + side, :]  50.9 us
    all_to_all x1, waiting for transfers between devices, body(): lax.all_to_all(jnp.stack(jnp.split(reduce_weight, lax.axis_size('chan'),...  37.2 us
    dot_general x9, matrix products, body(): total = total + jnp.dot(window, block, preferred_element_type=jnp.float32)  24.4 us
    slice x1, local copies, waits for them, and re-layouts, body(): padded[:, row_tap:row_tap + side, col_tap:col_tap + side, :]  23.7 us
  transfers between devices with their start and end apart: 4, of which 4 were waited for; matrix products, arithmetic and copies ran while one was open for 2% of the time, Pallas kernels for 0%

profile of v1, /device:TPU:0, one launch (start us, length us, event | category | flops | bytes accessed | tf_op | source)
XLA Modules:
  0.0 548.0 jit_solution(7141727104929392728)
XLA Ops:
  18.7 6.3 %all-to-all-start = ((bf16[4,1024,256]{1,2,0:T(8,128)(2,1)}), bf16[4,1024,256]{1,2,0:T(8,128)(2,1)}, u32[]{:S(2)}, u32[]{:S(2)}) async-start(bf16[4,1024,256]{1,2,0:T(8,128)(2,1)} %pad_maximum_fusion), calls=%async_computation | async-start | bytes 4194304 | tf_op jit(solution)/shard_map/all_to_all | solution.py:40
  25.1 5.5 %copy.17 = bf16[8,14,14,1024]{3,2,1,0:T(8,128)(2,1)} copy(bf16[8,14,14,1024]{3,0,2,1:T(8,128)(2,1)} %param.10) | data formatting | bytes 6422528 | tf_op args[0]
  30.5 5.6 %reshape.54 = bf16[1568,1024]{1,0:T(8,128)(2,1)} reshape(bf16[8,14,14,1024]{3,2,1,0:T(8,128)(2,1)} %copy.17) | data formatting | bytes 6422528 | tf_op jit(solution)/shard_map/reshape | solution.py:46
  36.2 37.2 %all-to-all-done = bf16[4,1024,256]{1,2,0:T(8,128)(2,1)} async-done(((bf16[4,1024,256]{1,2,0:T(8,128)(2,1)}), bf16[4,1024,256]{1,2,0:T(8,128)(2,1)}, u32[]{:S(2)}, u32[]{:S(2)}) %all-to-all-start) | async-done | bytes 2097184 | tf_op jit(solution)/shard_map/all_to_all | solution.py:40
  73.4 8.8 %convolution_bitcast_fusion = f32[1568,1024]{1,0:T(8,128)} fusion(bf16[1024,1024]{0,1:T(8,128)(2,1)} %bitcast.5, bf16[1568,1024]{1,0:T(8,128)(2,1)} %reshape.54), kind=kOutput, calls=%fused_computation.2 | convolution fusion | flops 3288334336 | bytes 11730944 | tf_op jit(solution)/shard_map/dot_general | solution.py:45
  82.2 112.1 %reduce-scatter.2.cloned.1.call-done = f32[1568,256]{1,0:T(8,128)} async-done(((f32[1568,1024]{1,0:T(8,128)}), f32[1568,256]{1,0:T(8,128)}) %reduce-scatter.2.cloned.1.call-update) | async-done | bytes 1605648 | tf_op jit(solution)/shard_map/reduce_scatter | solution.py:48
  195.9 13.6 %psum.42 = f32[256]{0:T(256)S(1)} all-reduce(f32[256]{0:T(256)S(1)} %reduce_sum.54), channel_id=1, replica_groups=mesh['batch'=8,'chan'=4] {'batch'}, use_global_device_ids=true, to_apply=%region_2.0 | all-reduce | flops 256 | bytes 2048 | tf_op jit(solution)/shard_map/psum | solution.py:10
  211.2 11.8 %psum.43 = f32[256]{0:T(256)S(1)} all-reduce(f32[256]{0:T(256)S(1)} %multiply_reduce_fusion.2), channel_id=1, replica_groups=mesh['batch'=8,'chan'=4] {'batch'}, use_global_device_ids=true, to_apply=%region_4.0 | all-reduce | flops 256 | bytes 2048 | tf_op jit(solution)/shard_map/psum | solution.py:10
  226.1 70.5 %all-gather.3.cloned.1.call-done = bf16[8,14,14,1024]{3,2,1,0:T(8,128)(2,1)} async-done(((bf16[8,14,14,256]{3,2,1,0:T(8,128)(2,1)}), bf16[8,14,14,1024]{3,2,1,0:T(8,128)(2,1)}) %all-gather.3.cloned.1.call-update) | async-done | bytes 3211280 | tf_op jit(solution)/shard_map/all_gather | solution.py:54
  296.6 23.7 %pad_slice_fusion = (bf16[8,14,14,1024]{3,2,1,0:T(8,128)(2,1)}, bf16[8,14,14,1024]{3,2,1,0:T(8,128)(2,1)}, bf16[8,14,14,1024]{3,2,1,0:T(8,128)(2,1)}, bf16[8,14,...) fusion(bf16[8,14,14,1024]{3,2,1,0:T(8,128)(2,1)} %all-gather.3., ...), kind=kLoop, calls=%fused_computation.11 | loop fusion | bytes 28901376 | tf_op jit(solution)/shard_map/slice | solution.py:59
  320.4 5.7 %reshape.64 = bf16[1568,1024]{1,0:T(8,128)(2,1)} reshape(bf16[8,14,14,1024]{3,2,1,0:T(8,128)(2,1)} %get-tuple-element.5) | data formatting | bytes 6422528 | tf_op jit(solution)/shard_map/reshape | solution.py:59
  326.1 5.7 %reshape.57 = bf16[1568,1024]{1,0:T(8,128)(2,1)} reshape(bf16[8,14,14,1024]{3,2,1,0:T(8,128)(2,1)} %get-tuple-element.6) | data formatting | bytes 6422528 | tf_op jit(solution)/shard_map/reshape | solution.py:59
  331.7 5.6 %reshape.58 = bf16[1568,1024]{1,0:T(8,128)(2,1)} reshape(bf16[8,14,14,1024]{3,2,1,0:T(8,128)(2,1)} %get-tuple-element.7) | data formatting | bytes 6422528 | tf_op jit(solution)/shard_map/reshape | solution.py:59
  337.4 5.7 %reshape.59 = bf16[1568,1024]{1,0:T(8,128)(2,1)} reshape(bf16[8,14,14,1024]{3,2,1,0:T(8,128)(2,1)} %get-tuple-element.8) | data formatting | bytes 6422528 | tf_op jit(solution)/shard_map/reshape | solution.py:59
  343.1 5.7 %reshape.61 = bf16[1568,1024]{1,0:T(8,128)(2,1)} reshape(bf16[8,14,14,1024]{3,2,1,0:T(8,128)(2,1)} %get-tuple-element.9) | data formatting | bytes 6422528 | tf_op jit(solution)/shard_map/reshape | solution.py:59
  348.7 5.6 %reshape.62 = bf16[1568,1024]{1,0:T(8,128)(2,1)} reshape(bf16[8,14,14,1024]{3,2,1,0:T(8,128)(2,1)} %get-tuple-element.10) | data formatting | bytes 6422528 | tf_op jit(solution)/shard_map/reshape | solution.py:59
  354.3 5.6 %reshape.63 = bf16[1568,1024]{1,0:T(8,128)(2,1)} reshape(bf16[8,14,14,1024]{3,2,1,0:T(8,128)(2,1)} %get-tuple-element.11) | data formatting | bytes 6422528 | tf_op jit(solution)/shard_map/reshape | solution.py:59
  360.0 5.7 %reshape.56 = bf16[1568,1024]{1,0:T(8,128)(2,1)} reshape(bf16[8,14,14,1024]{3,2,1,0:T(8,128)(2,1)} %get-tuple-element.12) | data formatting | bytes 6422528 | tf_op jit(solution)/shard_map/reshape | solution.py:59
  373.3 3.3 convolution_add_fusion.5
  376.5 5.6 %reshape.60 = bf16[1568,1024]{1,0:T(8,128)(2,1)} reshape(bf16[8,14,14,1024]{3,2,1,0:T(8,128)(2,1)} %all-gather.3.cloned.1.call-done) | data formatting | bytes 6422528 | tf_op jit(solution)/shard_map/reshape | solution.py:59
  382.2 3.7 convolution_add_fusion.4
  392.6 3.3 fusion.20
  395.8 13.6 %psum.44 = f32[256]{0:T(256)S(1)} all-reduce(f32[256]{0:T(256)S(1)} %get-tuple-element.17), channel_id=1, replica_groups=mesh['batch'=8,'chan'=4] {'batch'}, use_global_device_ids=true, to_apply=%region_6.7 | all-reduce | flops 256 | bytes 2048 | tf_op jit(solution)/shard_map/psum | solution.py:10
  411.2 11.8 %psum.45 = f32[256]{0:T(256)S(1)} all-reduce(f32[256]{0:T(256)S(1)} %multiply_reduce_fusion.1), channel_id=1, replica_groups=mesh['batch'=8,'chan'=4] {'batch'}, use_global_device_ids=true, to_apply=%region_8.9 | all-reduce | flops 256 | bytes 2048 | tf_op jit(solution)/shard_map/psum | solution.py:10
  425.5 60.9 %all-gather.5.cloned.1.call-done = bf16[1568,1024]{1,0:T(8,128)(2,1)} async-done(((bf16[1568,256]{1,0:T(8,128)(2,1)}), bf16[1568,1024]{1,0:T(8,128)(2,1)}) %all-gather.5.cloned.1.call-update) | async-done | bytes 3211280 | tf_op jit(solution)/shard_map/all_gather | solution.py:69
  486.5 7.4 %fusion.21 = (f32[1024]{0:T(1024)S(1)}, f32[1568,1024]{1,0:T(8,128)}) fusion(bf16[1568,1024]{1,0:T(8,128)(2,1)} %all-gather.5.cloned.1.call-done, bf16[1024,1024]{1,0:T(8,128)(2,1)S(1)} %copy-done), kind=kOutput, calls=%fused_computation.51 | convolution fusion | flops 3289938944 | bytes 11735040 | tf_op jit(solution)/shard_map/dot_general | solution.py:68
  493.9 13.6 %psum.46 = f32[1024]{0:T(1024)S(1)} all-reduce(f32[1024]{0:T(1024)S(1)} %get-tuple-element.19), channel_id=1, replica_groups=mesh['batch'=8,'chan'=4] {'batch'}, use_global_device_ids=true, to_apply=%region_10.11 | all-reduce | flops 1024 | bytes 8192 | tf_op jit(solution)/shard_map/psum | solution.py:10
  507.5 3.5 multiply_reduce_fusion
  511.1 11.8 %psum.47 = f32[1024]{0:T(1024)S(1)} all-reduce(f32[1024]{0:T(1024)S(1)} %multiply_reduce_fusion), channel_id=1, replica_groups=mesh['batch'=8,'chan'=4] {'batch'}, use_global_device_ids=true, to_apply=%region_12.13 | all-reduce | flops 1024 | bytes 8192 | tf_op jit(solution)/shard_map/psum | solution.py:10
  522.9 7.0 %maximum_convert_fusion = bf16[1568,1024]{1,0:T(8,128)(2,1)} fusion(bf16[1568,1024]{1,0:T(8,128)(2,1)} %reshape.54, f32[1568,1024]{1,0:T(8,128)} %get-tuple-element.20, f32[1024]{0:T(1024)S(1)} %copy-done.8, f32[1024]{0:T(1024)S(1)} %rsqrt_multiply_fusion, f32[1024]{0:T(1024)S(1)} %broadcast_multiply_fusion), kind=kLoop, calls=%fused_computation | loop fusion | flops 11239424 | bytes 12857344 | tf_op jit(solution)/shard_map/convert_element_type | solution.py:75
  529.8 5.6 %reshape.65 = bf16[8,14,14,1024]{3,2,1,0:T(8,128)(2,1)} reshape(bf16[1568,1024]{1,0:T(8,128)(2,1)} %maximum_convert_fusion) | data formatting | bytes 6422528 | tf_op jit(solution)/shard_map/reshape | solution.py:75
  535.5 6.0 %copy.18 = bf16[8,14,14,1024]{3,0,2,1:T(8,128)(2,1)} copy(bf16[8,14,14,1024]{3,2,1,0:T(8,128)(2,1)} %reshape.65) | data formatting | bytes 6422528 | tf_op jit(solution)/shard_map/reshape | solution.py:75
  (58 shorter events, 37.1 us)
Async XLA Ops:
  6.5 480.0 %copy-start = (bf16[1024,1024]{1,0:T(8,128)(2,1)S(1)}, bf16[1024,1024]{1,0:T(8,128)(2,1)}, u32[]{:S(2)}) copy-start(bf16[1024,1024]{1,0:T(8,128)(2,1)} %param.17) | copy-start | bytes 6291460
  18.7 54.6 %all-to-all-start = ((bf16[4,1024,256]{1,2,0:T(8,128)(2,1)}), bf16[4,1024,256]{1,2,0:T(8,128)(2,1)}, u32[]{:S(2)}, u32[]{:S(2)}) async-start(bf16[4,1024,256]{1,2,0:T(8,128)(2,1)} %pad_maximum_fusion), calls=%async_computation | async-start | bytes 4194304 | tf_op jit(solution)/shard_map/all_to_all | solution.py:40
  25.1 169.3 %reduce-scatter.2.cloned.1.call-start = ((), (), s32[]{:S(2)}) async-start(), calls=%async_computation.2 | async-start | bytes 8028160 | tf_op jit(solution)/shard_map/reduce_scatter | solution.py:48
  82.2 140.9 %copy-start.12 = (f32[256]{0:T(256)S(1)}, f32[256]{0:T(256)}, u32[]{:S(2)}) copy-start(f32[256]{0:T(256)} %param.12) | copy-start | bytes 3076
  82.2 140.8 %copy-start.10 = (f32[256]{0:T(256)S(1)}, f32[256]{0:T(256)}, u32[]{:S(2)}) copy-start(f32[256]{0:T(256)} %param.13) | copy-start | bytes 3076
  82.2 214.4 %all-gather.3.cloned.1.call-start = ((), (), s32[]{:S(2)}) async-start(), calls=%async_computation.3 | async-start | bytes 4587520 | tf_op jit(solution)/shard_map/all_gather | solution.py:54
  225.9 260.6 %all-gather.5.cloned.1.call-start = ((), (), s32[]{:S(2)}) async-start(), calls=%async_computation.4 | async-start | bytes 4014080 | tf_op jit(solution)/shard_map/all_gather | solution.py:69
  365.6 3.2 copy-start.7
  368.8 2.2 copy-start.6
  371.0 2.2 copy-start.5
  382.2 3.7 copy-start.4
  385.9 2.2 copy-start.3
  388.1 2.2 copy-start.2
  390.3 2.2 copy-start.1
  392.6 30.4 %copy-start.13 = (f32[256]{0:T(256)S(1)}, f32[256]{0:T(256)}, u32[]{:S(2)}) copy-start(f32[256]{0:T(256)} %param.15) | copy-start | bytes 3076
  392.6 30.4 %copy-start.11 = (f32[256]{0:T(256)S(1)}, f32[256]{0:T(256)}, u32[]{:S(2)}) copy-start(f32[256]{0:T(256)} %param.16) | copy-start | bytes 3076
  507.5 15.4 %copy-start.9 = (f32[1024]{0:T(1024)S(1)}, f32[1024]{0:T(1024)}, u32[]{:S(2)}) copy-start(f32[1024]{0:T(1024)} %param.18) | copy-start | bytes 12292
  507.5 15.4 %copy-start.8 = (f32[1024]{0:T(1024)S(1)}, f32[1024]{0:T(1024)}, u32[]{:S(2)}) copy-start(f32[1024]{0:T(1024)} %param.19) | copy-start | bytes 12292
Sparse Core Ops, SparseCore 0:
  82.3 111.9 reduce-scatter.1
  226.0 70.5 all-gather.2
  425.7 60.7 all-gather.4
